TPU v7x, 32 devices: a whole 2x2x4 slice. The times are simulated.
32 devices in a mesh: grp: 4 (over x, core), sub: 8 (over z, y).
Axes of the slice: x: 2, y: 2, z: 4, core: 2. Of those that a mesh axis runs over, the one named last changes fastest.
Arguments:
- snapshots: bfloat16 [2048, 2, 32, 128], P(None, None, ('grp', 'sub')), may hold values from -6 to 6
- steering: bfloat16 [32, 2, 128, 64], P(('grp', 'sub')), may hold values from -0.375 to 0.375
- combining: bfloat16 [32, 2, 64, 1024], P(('grp', 'sub')), may hold values from -0.09375 to 0.09375
- beam_list: int32 [1024], replicated, may hold values from 0 to 1023, each once
Outputs:
- beams_out: bfloat16 [2, 2048, 1024], P(None, ('grp', 'sub'))
Inputs may be any that keep to these rules, and one draw needn't show every extreme that they name: `beam_list`: each of the 1024 beams appears once.
All inputs are finite; a program needn't handle non-finite values.
Results may differ from a plain program's by a relative error of at most 0.0065.
Values may be sent and summed in bfloat16 or wider, within the bound.
A program may use at most 128 MiB of HBM per device.

v0:
```python
import functools

import jax
import jax.numpy as jnp
from jax import lax
from jax.experimental import pallas as pl
from jax.experimental.pallas import tpu as pltpu
from jax.sharding import PartitionSpec as P

MESH = pl.DeviceIdType.MESH
F32 = jnp.float32
BF16 = jnp.bfloat16
LAG = 2


class Plan:
    def __init__(self, mesh, snap, width, beams):
        self.grp = mesh.shape["grp"]
        self.sub = mesh.shape["sub"]
        self.cores = 2 if self.grp % 2 == 0 else 1
        self.nx = self.grp // self.cores
        self.halves, self.pair = (2, 2) if self.sub % 4 == 0 else (1, 1)
        self.hi = self.halves * self.pair
        self.lo = self.sub // self.hi
        self.block = snap // (self.grp * self.sub)
        self.width = width
        self.beams = beams
        self.chunks = 8 if beams % 1024 == 0 else 1
        self.cols = beams // self.chunks
        self.offsets = [(dx, dy) for dx in range(self.nx) for dy in range(self.lo)]
        self.slots = len(self.offsets) * self.cores


def beam_kernel(
    plan,
    x_hbm,
    s_ref,
    w_hbm,
    list_ref,
    out_ref,
    x_ref,
    w_ref,
    in_sem,
    even_buf,
    odd_buf,
    pall,
    pbuf,
    lhs_buf,
    wbuf,
    own_buf,
    share_buf,
    merged_buf,
    got_buf,
    pick_buf,
    acc_buf,
    psend,
    precv,
    wsend,
    wrecv,
    ssend,
    srecv,
):
    cores, nx, lo, hi = plan.cores, plan.nx, plan.lo, plan.hi
    halves, pair = plan.halves, plan.pair
    cols, width, block = plan.cols, plan.width, plan.block
    half = width // 2
    offsets = plan.offsets
    count = len(offsets)
    g = lax.axis_index("grp")
    s = lax.axis_index("sub")
    core, xi = lax.rem(g, cores), lax.div(g, cores)
    z, y = lax.div(s, lo), lax.rem(s, lo)
    zh, zl = lax.div(z, pair), lax.rem(z, pair)

    def peer(dx, dy, dc):
        gg = lax.rem(xi + dx, nx) * cores + lax.rem(core + dc, cores)
        yy = lax.rem(y + dy, lo)
        return gg, yy

    def slot(o, dc):
        return dc * count + o

    plane = [(o, dc) for o in range(count) for dc in range(cores) if (o, dc) != (0, 0)]
    plane.sort(key=lambda item: -sum(1 for v in offsets[item[0]] if v))

    load_w = pltpu.make_async_copy(w_hbm, w_ref, in_sem.at[0])
    load_w.start()
    load_x = pltpu.make_async_copy(x_hbm, x_ref, in_sem.at[1])
    load_x.start()
    barrier = pltpu.get_barrier_semaphore()
    for o, dc in plane:
        gg, yy = peer(*offsets[o], dc)
        pl.semaphore_signal(barrier, inc=1, device_id=(gg, z * lo + yy), device_id_type=MESH)
    if hi > 1:
        near = (g, (2 * zh + 1 - zl) * lo + y)
        far = (g, (2 * (1 - zh) + zl) * lo + y)
        for target in (near, far):
            pl.semaphore_signal(barrier, inc=1, device_id=target, device_id_type=MESH)
    pl.semaphore_wait(barrier, len(plane) + (2 if hi > 1 else 0))

    def w_columns(c):
        return w_ref.at[:, pl.ds(c * cols, cols)]

    sends = []

    def send_w(c):
        for o in sorted(range(count), key=lambda o: -sum(1 for v in offsets[o] if v)):
            if o == 0:
                if cores > 1:
                    gg, yy = peer(0, 0, 1)
                    k = slot(0, 1)
                else:
                    continue
            else:
                gg, yy = peer(*offsets[o], 0)
                k = slot(o, 0)
            copy = pltpu.make_async_remote_copy(
                src_ref=w_columns(c),
                dst_ref=wbuf.at[c, k],
                send_sem=wsend.at[c, k],
                recv_sem=wrecv.at[c, k],
                device_id=(gg, z * lo + yy),
                device_id_type=MESH,
            )
            copy.start()
            sends.append(copy)

    def relay_w(c):
        if cores == 1:
            return
        gg, yy = peer(0, 0, 1)
        for o in range(1, count):
            wait_w(c, slot(o, 0))
            copy = pltpu.make_async_remote_copy(
                src_ref=wbuf.at[c, slot(o, 0)],
                dst_ref=wbuf.at[c, slot(o, 1)],
                send_sem=wsend.at[c, slot(o, 1)],
                recv_sem=wrecv.at[c, slot(o, 1)],
                device_id=(gg, z * lo + yy),
                device_id_type=MESH,
            )
            copy.start()
            sends.append(copy)

    def wait_w(c, k):
        pltpu.make_async_copy(wbuf.at[c, k], wbuf.at[c, k], wrecv.at[c, k]).wait()

    load_w.wait()
    send_w(0)
    load_x.wait()

    upper = s_ref[...]
    lower = jnp.concatenate([-upper[half:], upper[:half]], axis=0)
    rows_g = hi * lo * block
    contract = (((1,), (1,)), ((), ()))
    for gg in range(plan.grp):
        part = x_ref[pl.ds(gg * rows_g * 2, rows_g * 2), :]
        even_buf[...] = lax.dot_general(part, upper, contract, preferred_element_type=F32)
        odd_buf[...] = lax.dot_general(part, lower, contract, preferred_element_type=F32)
        value = even_buf[pl.ds(0, rows_g, stride=2), :] + odd_buf[pl.ds(1, rows_g, stride=2), :]
        pall[gg] = value.reshape(halves, pair, lo, block, width).astype(BF16)

    def half_of(h):
        return zh if h == halves - 1 else 1 - zh

    def send_p(h):
        for o, dc in plane:
            gg, yy = peer(*offsets[o], dc)
            k = slot(o, dc)
            copy = pltpu.make_async_remote_copy(
                src_ref=pall.at[gg, half_of(h), :, yy],
                dst_ref=pbuf.at[h, k],
                send_sem=psend.at[h, k],
                recv_sem=precv.at[h, k],
                device_id=(gg, z * lo + yy),
                device_id_type=MESH,
            )
            copy.start()
            sends.append(copy)

    def wait_p(h):
        own = pall[g, half_of(h), :, y]
        lhs_buf[h, :, pl.ds(0, width)] = own.reshape(pair * block, width)
        for o, dc in reversed(plane):
            k = slot(o, dc)
            pltpu.make_async_copy(pbuf.at[h, k], pbuf.at[h, k], precv.at[h, k]).wait()
            lhs_buf[h, :, pl.ds(k * width, width)] = pbuf[h, k].reshape(pair * block, width)

    send_p(0)
    for c in range(1, 3):
        send_w(c)

    for c in range(plan.chunks):
        row = lax.broadcasted_iota(jnp.int32, (cols, plan.beams), 0) + c * cols
        pick_buf[pl.ds(c * cols, cols), :] = jnp.where(row == list_ref[...], 1.0, 0.0).astype(BF16)
        wbuf[c, 0] = w_ref[:, pl.ds(c * cols, cols)]

    relay_w(0)
    wait_p(0)

    def share(c, k, source, target):
        copy = pltpu.make_async_remote_copy(
            src_ref=source,
            dst_ref=got_buf.at[c, k],
            send_sem=ssend.at[c, k],
            recv_sem=srecv.at[c, k],
            device_id=target,
            device_id_type=MESH,
        )
        copy.start()
        sends.append(copy)

    def wait_share(c, k):
        pltpu.make_async_copy(got_buf.at[c, k], got_buf.at[c, k], srecv.at[c, k]).wait()

    def merge(c):
        if hi == 1:
            return
        wait_share(c, 0)
        merged_buf[c] = (own_buf[0, c, zl] + got_buf[c, 0].astype(F32)).astype(BF16)
        share(c, 2, merged_buf.at[c], far)

    def finish(c):
        total = own_buf[halves - 1, c, zl]
        if hi > 1:
            for k in (1, 2):
                wait_share(c, k)
                total = total + got_buf[c, k].astype(F32)
        rounded = total.astype(BF16).reshape(2 * block, cols)
        placed = jnp.dot(rounded, pick_buf[pl.ds(c * cols, cols), :], preferred_element_type=F32)
        if c == 0:
            acc_buf[...] = placed
        else:
            acc_buf[...] += placed

    def multiply(h, c):
        weights = wbuf[c]
        w_real, w_imag = weights[:, :half], weights[:, half:]
        for part, rhs in enumerate(((w_real, -w_imag), (w_imag, w_real))):
            rhs = jnp.concatenate(rhs, axis=1).reshape(plan.slots * width, cols)
            value = jnp.dot(lhs_buf[h], rhs, preferred_element_type=F32)
            value = value.reshape(pair, block, cols)
            own_buf[h, c, :, part] = value
            share_buf[h, c, :, part] = value.astype(BF16)
        if hi > 1:
            share(c, h, share_buf.at[h, c, 1 - zl], near)

    for c in range(plan.chunks):
        if c + 3 < plan.chunks:
            send_w(c + 3)
        if c == plan.chunks - 3:
            send_p(1)
        for o in range(count):
            if cores > 1:
                wait_w(c, slot(o, 1))
            elif o > 0:
                wait_w(c, slot(o, 0))
        multiply(0, c)
        if c + 1 < plan.chunks:
            relay_w(c + 1)
        if c >= LAG:
            merge(c - LAG)
    for c in range(max(plan.chunks - LAG, 0), plan.chunks):
        merge(c)
    for h in range(1, halves):
        wait_p(h)
        for c in range(plan.chunks):
            multiply(h, c)
    for c in range(plan.chunks):
        finish(c)
    out_ref[...] = acc_buf[...].astype(BF16).reshape(2, block, plan.beams)
    for copy in sends:
        copy.wait_send()


def shards(plan, snapshots, steering, combining, beam_list):
    snap, _, _, elements = snapshots.shape
    signal = snapshots.reshape(snap * 2, elements)
    steer = jnp.transpose(steering[0], (0, 2, 1)).reshape(plan.width, elements)
    weights = combining.reshape(plan.width, plan.beams)
    rows_g = plan.hi * plan.lo * plan.block
    line = (plan.halves, plan.pair)
    vmem = pl.BlockSpec(memory_space=pltpu.VMEM)
    hbm = pl.BlockSpec(memory_space=pl.ANY)
    dma = pltpu.SemaphoreType.DMA
    return pl.pallas_call(
        functools.partial(beam_kernel, plan),
        out_shape=jax.ShapeDtypeStruct((2, plan.block, plan.beams), BF16),
        in_specs=[hbm, vmem, hbm, vmem],
        out_specs=vmem,
        scratch_shapes=[
            pltpu.VMEM(signal.shape, BF16),
            pltpu.VMEM(weights.shape, BF16),
            dma((2,)),
            pltpu.VMEM((rows_g * 2, plan.width), F32),
            pltpu.VMEM((rows_g * 2, plan.width), F32),
            pltpu.VMEM((plan.grp, *line, plan.lo, plan.block, plan.width), BF16),
            pltpu.VMEM((plan.halves, plan.slots, plan.pair, plan.block, plan.width), BF16),
            pltpu.VMEM((plan.halves, plan.pair * plan.block, plan.slots * plan.width), BF16),
            pltpu.VMEM((plan.chunks, plan.slots, plan.width, plan.cols), BF16),
            pltpu.VMEM((plan.halves, plan.chunks, plan.pair, 2, plan.block, plan.cols), F32),
            pltpu.VMEM((plan.halves, plan.chunks, plan.pair, 2, plan.block, plan.cols), BF16),
            pltpu.VMEM((plan.chunks, 2, plan.block, plan.cols), BF16),
            pltpu.VMEM((plan.chunks, 3, 2, plan.block, plan.cols), BF16),
            pltpu.VMEM((plan.beams, plan.beams), BF16),
            pltpu.VMEM((2 * plan.block, plan.beams), F32),
            dma((plan.halves, plan.slots)),
            dma((plan.halves, plan.slots)),
            dma((plan.chunks, plan.slots)),
            dma((plan.chunks, plan.slots)),
            dma((plan.chunks, 3)),
            dma((plan.chunks, 3)),
        ],
        compiler_params=pltpu.CompilerParams(
            collective_id=0, has_side_effects=True, vmem_limit_bytes=60 * 1024 * 1024
        ),
    )(signal, steer, weights, beam_list.reshape(1, plan.beams))


def solution(mesh):
    placed = (
        P(None, None, ("grp", "sub"), None),
        P(("grp", "sub"), None, None, None),
        P(("grp", "sub"), None, None, None),
        P(),
    )

    def whole(snapshots, steering, combining, beam_list):
        plan = Plan(mesh, snapshots.shape[0], 2 * steering.shape[3], combining.shape[3])
        return jax.shard_map(
            functools.partial(shards, plan),
            mesh=mesh,
            in_specs=placed,
            out_specs=P(None, ("grp", "sub"), None),
            check_vma=False,
        )(snapshots, steering, combining, beam_list)

    return whole
```

profile of v0, /device:TPU:0, one launch (start us, length us, event | category | flops | bytes accessed | tf_op | source)
XLA Modules:
  0.0 39.9 jit_solution(268174324823724684)
XLA Ops:
  0.0 38.2 %shard_map.46 = bf16[2,64,1024]{2,1,0:T(8,128)(2,1)} custom-call(bf16[4096,128]{1,0:T(8,128)(2,1)} %bitcast.8, bf16[128,128]{1,0:T(8,128)(2,1)} %bitcast.10, bf16[128,1024]{1,0:T(8,128)(2,1)} %bitcast.9, s32[1,1024]{1,0:T(1,128)} %bitcast.11), custom_call_target="tpu_custom_call" | custom-call | tf_op jit(solution)/shard_map/pallas_call | solution.py:286
  38.2 1.7 %copy.6 = bf16[2,64,1024]{2,1,0:T(8,128)(2,1)} copy(bf16[2,64,1024]{2,1,0:T(8,128)(2,1)} %shard_map.46) | data formatting | bytes 524288
where the time goes:
time: 40.1 us; the launch traced here: 39.9 us
  Pallas kernels  38.2 us (95%)
  local copies, waits for them, and re-layouts  1.67 us (4%)
    pallas_call x1, Pallas kernels, shards(): pl.pallas_call(functools.partial(beam_kernel, plan), out_shape=jax.ShapeD...  38.2 us
    unnamed x1, local copies, waits for them, and re-layouts  1.67 us

commit v1 on v0

v1 whole, which is shorter than its diff:
```python
import functools

import jax
import jax.numpy as jnp
from jax import lax
from jax.experimental import pallas as pl
from jax.experimental.pallas import tpu as pltpu
from jax.sharding import PartitionSpec as P

MESH = pl.DeviceIdType.MESH
F32 = jnp.float32
BF16 = jnp.bfloat16
LAG = 3
AHEAD = 3
SECOND = 3
VMEM_LIMIT = 63 * 1024 * 1024


class Plan:
    def __init__(self, mesh, snap, width, beams):
        self.grp = mesh.shape["grp"]
        self.sub = mesh.shape["sub"]
        self.cores = 2 if self.grp % 2 == 0 else 1
        self.nx = self.grp // self.cores
        self.halves, self.pair = 2, 2
        self.hi = self.halves * self.pair
        self.lo = self.sub // self.hi
        self.block = snap // (self.grp * self.sub)
        self.width = width
        self.beams = beams
        self.chunks = 8 if beams % 1024 == 0 else 1
        self.cols = beams // self.chunks
        self.offsets = [(dx, dy) for dx in range(self.nx) for dy in range(self.lo)]
        self.slots = len(self.offsets) * self.cores
        self.rows_h = self.pair * self.lo * self.block


def beam_kernel(
    plan,
    x_hbm,
    s_hbm,
    w_hbm,
    list_hbm,
    out_ref,
    x_ref,
    s_ref,
    list_ref,
    in_sem,
    x_sem,
    w_sem,
    even_buf,
    odd_buf,
    pall,
    pbuf,
    lhs_buf,
    wbuf,
    own_buf,
    share_buf,
    merged_buf,
    near_buf,
    got_buf,
    pick_buf,
    acc_buf,
    psend,
    precv,
    wsend,
    wrecv,
    ssend,
    srecv,
    msend,
    mrecv,
    nsend,
    nrecv,
):
    cores, nx, lo, hi = plan.cores, plan.nx, plan.lo, plan.hi
    halves, pair, chunks = plan.halves, plan.pair, plan.chunks
    cols, width, block = plan.cols, plan.width, plan.block
    half = width // 2
    offsets = plan.offsets
    count = len(offsets)
    g = lax.axis_index("grp")
    s = lax.axis_index("sub")
    core, xi = lax.rem(g, cores), lax.div(g, cores)
    z, y = lax.div(s, lo), lax.rem(s, lo)
    zh, zl = lax.div(z, pair), lax.rem(z, pair)
    is_end = zh == zl
    is_mid = zh != zl

    def peer(dx, dy, dc):
        gg = lax.rem(xi + dx, nx) * cores + lax.rem(core + dc, cores)
        yy = lax.rem(y + dy, lo)
        return gg, yy

    def level(zz):
        return (g, zz * lo + y)

    def half_of(h):
        return zh if h == halves - 1 else 1 - zh

    def slot(o, dc):
        return dc * count + o

    def hops(o):
        return sum(1 for v in offsets[o] if v)

    plane = [(o, dc) for o in range(count) for dc in range(cores) if (o, dc) != (0, 0)]
    plane.sort(key=lambda item: -hops(item[0]))

    load_s = pltpu.make_async_copy(s_hbm, s_ref, in_sem.at[0])
    load_s.start()

    def x_copy(h, gg):
        start = (gg * hi + half_of(h) * pair) * lo * block * 2
        return pltpu.make_async_copy(
            x_hbm.at[pl.ds(pl.multiple_of(start, 16), plan.rows_h * 2), :], x_ref.at[h, gg], x_sem.at[h, gg]
        )

    def w_copy(c):
        return pltpu.make_async_copy(w_hbm.at[:, pl.ds(c * cols, cols)], wbuf.at[c, 0], w_sem.at[c])

    for gg in range(plan.grp):
        x_copy(0, gg).start()
    for c in range(chunks):
        w_copy(c).start()
    for gg in range(plan.grp):
        x_copy(1, gg).start()
    load_list = pltpu.make_async_copy(list_hbm, list_ref, in_sem.at[1])
    load_list.start()

    barrier = pltpu.get_barrier_semaphore()
    for o, dc in plane:
        gg, yy = peer(*offsets[o], dc)
        pl.semaphore_signal(barrier, inc=1, device_id=(gg, z * lo + yy), device_id_type=MESH)
    near = level(zh * pair + 1 - zl)
    far_mid = level((1 - zh) * pair + zh)
    far_end = level((1 - zh) * pair + 1 - zh)
    pl.semaphore_signal(barrier, inc=1, device_id=near, device_id_type=MESH)
    pl.semaphore_signal(barrier, inc=1, device_id=far_mid, device_id_type=MESH)

    @pl.when(is_mid)
    def _():
        pl.semaphore_signal(barrier, inc=1, device_id=far_end, device_id_type=MESH)

    load_s.wait()
    upper = s_ref[...]
    both = jnp.concatenate([upper, -upper[half:], upper[:half]], axis=0)
    contract = (((1,), (1,)), ((), ()))

    def partial(h):
        for gg in range(plan.grp):
            x_copy(h, gg).wait()
            value = lax.dot_general(x_ref[h, gg], both, contract, preferred_element_type=F32)
            b = gg % 2
            even_buf[b] = value[:, :width]
            odd_buf[b] = value[:, width:]
            value = (
                even_buf[b, pl.ds(0, plan.rows_h, stride=2), :] + odd_buf[b, pl.ds(1, plan.rows_h, stride=2), :]
            )
            pall[h, gg] = value.reshape(pair, lo, block, width).astype(BF16)

    sends = []

    def remote(src, dst, send, recv, target):
        return pltpu.make_async_remote_copy(
            src_ref=src, dst_ref=dst, send_sem=send, recv_sem=recv, device_id=target, device_id_type=MESH
        )

    def arrived(ref, sem):
        pltpu.make_async_copy(ref, ref, sem).wait()

    def wait_w(c, k):
        arrived(wbuf.at[c, k], wrecv.at[c, k])

    def send_w(c):
        w_copy(c).wait()
        for o in sorted(range(count), key=lambda o: -hops(o)):
            if o == 0 and cores == 1:
                continue
            dc = 1 if o == 0 else 0
            gg, yy = peer(*offsets[o], dc)
            k = slot(o, dc)
            copy = remote(wbuf.at[c, 0], wbuf.at[c, k], wsend.at[c, k], wrecv.at[c, k], (gg, z * lo + yy))
            copy.start()
            sends.append(copy)

    def relay_w(c):
        if cores == 1:
            return
        gg, yy = peer(0, 0, 1)
        for o in sorted(range(1, count), key=hops):
            wait_w(c, slot(o, 0))
            k = slot(o, 1)
            copy = remote(wbuf.at[c, slot(o, 0)], wbuf.at[c, k], wsend.at[c, k], wrecv.at[c, k], (gg, z * lo + yy))
            copy.start()
            sends.append(copy)

    def ready_w(c):
        for o in range(count):
            if cores > 1:
                wait_w(c, slot(o, 1))
            elif o > 0:
                wait_w(c, slot(o, 0))

    def send_p(h):
        for o, dc in plane:
            gg, yy = peer(*offsets[o], dc)
            k = slot(o, dc)
            copy = remote(pall.at[h, gg, :, yy], pbuf.at[h, k], psend.at[h, k], precv.at[h, k], (gg, z * lo + yy))
            copy.start()
            sends.append(copy)

    sign = jnp.where(lax.broadcasted_iota(jnp.int32, (block, width), 1) < half, 1.0, -1.0).astype(F32)

    def place(h, k, value):
        for p in range(pair):
            rows = value[p].astype(F32)
            columns = pl.ds(k * width, width)
            lhs_buf[h, pl.ds(2 * p * block, block), columns] = (rows * sign).astype(BF16)
            turned = jnp.concatenate([rows[:, half:], rows[:, :half]], axis=1)
            lhs_buf[h, pl.ds((2 * p + 1) * block, block), columns] = turned.astype(BF16)

    def wait_p(h):
        place(h, 0, pall[h, g, :, y])
        for o, dc in reversed(plane):
            k = slot(o, dc)
            arrived(pbuf.at[h, k], precv.at[h, k])
            place(h, k, pbuf[h, k])

    def product(h, c):
        weights = wbuf[c].reshape(plan.slots * width, cols)
        value = jnp.dot(lhs_buf[h], weights, preferred_element_type=F32).reshape(pair, 2, block, cols)
        own_buf[h, c] = value
        share_buf[h, c] = value.astype(BF16)

    def to_near(c):
        return remote(share_buf.at[0, c], near_buf.at[c], nsend.at[c], nrecv.at[c], near)

    def to_owner(c, p):
        return remote(
            merged_buf.at[c, p], got_buf.at[c, 1], msend.at[c, p], mrecv.at[c], level((1 - zh) * pair + p)
        )

    def first(c):
        product(0, c)

        @pl.when(is_end)
        def _():
            to_near(c).start()

    def merge(c):
        @pl.when(is_mid)
        def _():
            arrived(near_buf.at[c], nrecv.at[c])
            merged_buf[c] = (own_buf[0, c] + near_buf[c].astype(F32)).astype(BF16)
            for p in range(pair):
                to_owner(c, p).start()

    def second(c):
        product(1, c)
        copy = remote(share_buf.at[1, c, 1 - zl], got_buf.at[c, 0], ssend.at[c], srecv.at[c], near)
        copy.start()
        sends.append(copy)

    def finish(c):
        arrived(got_buf.at[c, 1], mrecv.at[c])
        total = own_buf[1, c, zl] + got_buf[c, 1].astype(F32)
        arrived(got_buf.at[c, 0], srecv.at[c])
        total = total + got_buf[c, 0].astype(F32)
        rounded = total.astype(BF16).reshape(2 * block, cols)
        placed = jnp.dot(rounded, pick_buf[pl.ds(c * cols, cols), :], preferred_element_type=F32)
        if c == 0:
            acc_buf[...] = placed
        elif c < chunks - 1:
            acc_buf[...] += placed
        else:
            out_ref[...] = (acc_buf[...] + placed).astype(BF16).reshape(2, block, plan.beams)

    partial(0)
    pl.semaphore_wait(barrier, len(plane) + jnp.where(is_mid, 3, 2))
    send_w(0)
    send_p(0)
    for c in range(1, min(AHEAD, chunks)):
        send_w(c)
    partial(1)
    load_list.wait()
    for c in range(chunks):
        row = lax.broadcasted_iota(jnp.int32, (cols, plan.beams), 0) + c * cols
        pick_buf[pl.ds(c * cols, cols), :] = jnp.where(row == list_ref[...], 1.0, 0.0).astype(BF16)
    relay_w(0)
    wait_p(0)
    for c in range(chunks):
        if c + AHEAD < chunks:
            send_w(c + AHEAD)
        if c == min(SECOND, chunks - 1):
            send_p(1)
        if c + 1 < chunks:
            relay_w(c + 1)
        ready_w(c)
        first(c)
        if c >= LAG:
            merge(c - LAG)
    wait_p(1)
    left = list(range(max(chunks - LAG, 0), chunks))
    for c in range(chunks):
        second(c)
        if c % 2 == 1 and left:
            merge(left.pop(0))
    for c in left:
        merge(c)
    for c in range(chunks):
        finish(c)

    for copy in sends:
        copy.wait_send()

    @pl.when(is_end)
    def _():
        for c in range(chunks):
            to_near(c).wait_send()

    @pl.when(is_mid)
    def _():
        for c in range(chunks):
            for p in range(pair):
                to_owner(c, p).wait_send()


def shards(plan, snapshots, steering, combining, beam_list):
    snap, _, _, elements = snapshots.shape
    signal = snapshots.reshape(snap * 2, elements)
    steer = jnp.transpose(steering[0], (0, 2, 1)).reshape(plan.width, elements)
    weights = combining.reshape(plan.width, plan.beams)
    pair, block, cols, chunks, halves = plan.pair, plan.block, plan.cols, plan.chunks, plan.halves
    hbm = pl.BlockSpec(memory_space=pl.ANY)
    dma = pltpu.SemaphoreType.DMA
    return pl.pallas_call(
        functools.partial(beam_kernel, plan),
        out_shape=jax.ShapeDtypeStruct((2, block, plan.beams), BF16),
        in_specs=[hbm, hbm, hbm, hbm],
        out_specs=pl.BlockSpec(memory_space=pltpu.VMEM),
        scratch_shapes=[
            pltpu.VMEM((halves, plan.grp, plan.rows_h * 2, elements), BF16),
            pltpu.VMEM((plan.width, elements), BF16),
            pltpu.VMEM((1, plan.beams), jnp.int32),
            dma((2,)),
            dma((halves, plan.grp)),
            dma((chunks,)),
            pltpu.VMEM((2, plan.rows_h * 2, plan.width), F32),
            pltpu.VMEM((2, plan.rows_h * 2, plan.width), F32),
            pltpu.VMEM((halves, plan.grp, pair, plan.lo, block, plan.width), BF16),
            pltpu.VMEM((halves, plan.slots, pair, block, plan.width), BF16),
            pltpu.VMEM((halves, pair * 2 * block, plan.slots * plan.width), BF16),
            pltpu.VMEM((chunks, plan.slots, plan.width, cols), BF16),
            pltpu.VMEM((halves, chunks, pair, 2, block, cols), F32),
            pltpu.VMEM((halves, chunks, pair, 2, block, cols), BF16),
            pltpu.VMEM((chunks, pair, 2, block, cols), BF16),
            pltpu.VMEM((chunks, pair, 2, block, cols), BF16),
            pltpu.VMEM((chunks, 2, 2, block, cols), BF16),
            pltpu.VMEM((plan.beams, plan.beams), BF16),
            pltpu.VMEM((2 * block, plan.beams), F32),
            dma((halves, plan.slots)),
            dma((halves, plan.slots)),
            dma((chunks, plan.slots)),
            dma((chunks, plan.slots)),
            dma((chunks,)),
            dma((chunks,)),
            dma((chunks, pair)),
            dma((chunks,)),
            dma((chunks,)),
            dma((chunks,)),
        ],
        compiler_params=pltpu.CompilerParams(
            collective_id=0, has_side_effects=True, vmem_limit_bytes=VMEM_LIMIT
        ),
    )(signal, steer, weights, beam_list.reshape(1, plan.beams))


def solution(mesh):
    placed = (
        P(None, None, ("grp", "sub"), None),
        P(("grp", "sub"), None, None, None),
        P(("grp", "sub"), None, None, None),
        P(),
    )

    def whole(snapshots, steering, combining, beam_list):
        plan = Plan(mesh, snapshots.shape[0], 2 * steering.shape[3], combining.shape[3])
        return jax.shard_map(
            functools.partial(shards, plan),
            mesh=mesh,
            in_specs=placed,
            out_specs=P(None, ("grp", "sub"), None),
            check_vma=False,
        )(snapshots, steering, combining, beam_list)

    return whole
```

time: 40.1 us -> 42.3 us (1.055)
  Pallas kernels: 38.2 us -> 40.5 us
    pallas_call x1, Pallas kernels: 38.2 us -> 40.5 us  [shards(): pl.pallas_call(functools.partial(beam_kernel, plan), out_shape=jax.ShapeD...]
where the time goes in v1:
time: 42.3 us; the launch traced here: 42.2 us
  Pallas kernels  40.5 us (96%)
  local copies, waits for them, and re-layouts  1.67 us (4%)
    pallas_call x1, Pallas kernels, shards(): pl.pallas_call(functools.partial(beam_kernel, plan), out_shape=jax.ShapeD...  40.5 us
    unnamed x1, local copies, waits for them, and re-layouts  1.67 us

profile of v1, /device:TPU:0, one launch (start us, length us, event | category | flops | bytes accessed | tf_op | source)
XLA Modules:
  0.0 42.2 jit_solution(17539614223994910376)
XLA Ops:
  0.0 40.5 %shard_map.46 = bf16[2,64,1024]{2,1,0:T(8,128)(2,1)} custom-call(bf16[4096,128]{1,0:T(8,128)(2,1)} %bitcast.8, bf16[128,128]{1,0:T(8,128)(2,1)} %bitcast.10, bf16[128,1024]{1,0:T(8,128)(2,1)} %bitcast.9, s32[1,1024]{1,0:T(1,128)} %bitcast.11), custom_call_target="tpu_custom_call" | custom-call | tf_op jit(solution)/shard_map/pallas_call | solution.py:336
  40.5 1.7 %copy.6 = bf16[2,64,1024]{2,1,0:T(8,128)(2,1)} copy(bf16[2,64,1024]{2,1,0:T(8,128)(2,1)} %shard_map.46) | data formatting | bytes 524288

commit v2 on v1

v2 whole, which is shorter than its diff:
```python
import functools

import jax
import jax.numpy as jnp
from jax import lax
from jax.experimental import pallas as pl
from jax.experimental.pallas import tpu as pltpu
from jax.sharding import PartitionSpec as P

MESH = pl.DeviceIdType.MESH
F32 = jnp.float32
BF16 = jnp.bfloat16
AHEAD = 4
PRE = 1
END = [
    "W4",
    "W5",
    "W6",
    "W7",
    "X",
    "R0",
    "P0",
    "Y0",
    "F0",
    "R1",
    "Y1",
    "F1",
    "R2",
    "Y2",
    "F2",
    "R3",
    "Y3",
    "F3",
    "R4",
    "Y4",
    "F4",
    "R5",
    "Y5",
    "F5",
    "R6",
    "Y6",
    "F6",
    "R7",
    "Y7",
    "F7",
    "P1",
    "S0",
    "S1",
    "S2",
    "S3",
    "S4",
    "S5",
    "S6",
    "S7",
]
MID = [
    "W4",
    "X",
    "W5",
    "W6",
    "W7",
    "R0",
    "P0",
    "Y0",
    "F0",
    "R1",
    "Y1",
    "F1",
    "R2",
    "Y2",
    "F2",
    "M0",
    "R3",
    "Y3",
    "F3",
    "M1",
    "R4",
    "Y4",
    "F4",
    "M2",
    "P1",
    "S0",
    "M3",
    "R5",
    "S1",
    "M4",
    "S2",
    "Y5",
    "F5",
    "R6",
    "S3",
    "M5",
    "S4",
    "Y6",
    "F6",
    "R7",
    "S5",
    "M6",
    "S6",
    "Y7",
    "F7",
    "S7",
    "M7",
]
VMEM_LIMIT = 60 * 1024 * 1024


class Plan:
    def __init__(self, mesh, snap, width, beams):
        self.grp = mesh.shape["grp"]
        self.sub = mesh.shape["sub"]
        self.cores = 2 if self.grp % 2 == 0 else 1
        self.nx = self.grp // self.cores
        self.halves, self.pair = 2, 2
        self.hi = self.halves * self.pair
        self.lo = self.sub // self.hi
        self.block = snap // (self.grp * self.sub)
        self.width = width
        self.beams = beams
        self.chunks = 8 if beams % 1024 == 0 else 1
        self.cols = beams // self.chunks
        self.offsets = [(dx, dy) for dx in range(self.nx) for dy in range(self.lo)]
        self.slots = len(self.offsets) * self.cores
        self.rows_h = self.pair * self.lo * self.block

    def steps(self, steps):
        if self.chunks == 8:
            return steps
        plain = [f"W{c}" for c in range(min(AHEAD, self.chunks), self.chunks)] + ["X", "R0", "P0", "Y0", "F0"]
        for c in range(1, self.chunks):
            plain += [f"R{c}", f"Y{c}", f"F{c}"]
        plain += [f"M{c}" for c in range(self.chunks) if "M0" in steps] + ["P1"]
        return plain + [f"S{c}" for c in range(self.chunks)]


def beam_kernel(
    plan,
    x_hbm,
    s_hbm,
    w_hbm,
    list_hbm,
    out_ref,
    x_ref,
    s_ref,
    both_buf,
    list_ref,
    in_sem,
    w_sem,
    even_buf,
    odd_buf,
    pall,
    pbuf,
    lhs_buf,
    wbuf,
    own_buf,
    share_buf,
    pass_buf,
    last_buf,
    near_buf,
    got_buf,
    pick_buf,
    acc_buf,
    send_sem,
    precv,
    wrecv,
    srecv,
    mrecv,
    nrecv,
):
    cores, nx, lo, hi = plan.cores, plan.nx, plan.lo, plan.hi
    halves, pair, chunks = plan.halves, plan.pair, plan.chunks
    cols, width, block = plan.cols, plan.width, plan.block
    half = width // 2
    offsets = plan.offsets
    count = len(offsets)
    g = lax.axis_index("grp")
    s = lax.axis_index("sub")
    core, xi = lax.rem(g, cores), lax.div(g, cores)
    z, y = lax.div(s, lo), lax.rem(s, lo)
    zh, zl = lax.div(z, pair), lax.rem(z, pair)
    is_end = zh == zl
    is_mid = zh != zl

    def peer(dx, dy, dc):
        gg = lax.rem(xi + dx, nx) * cores + lax.rem(core + dc, cores)
        yy = lax.rem(y + dy, lo)
        return gg, yy

    def level(zz):
        return (g, zz * lo + y)

    def half_of(h):
        return zh if h == halves - 1 else 1 - zh

    def slot(o, dc):
        return dc * count + o

    def hops(o):
        return sum(1 for v in offsets[o] if v)

    plane = [(o, dc) for o in range(count) for dc in range(cores) if (o, dc) != (0, 0)]
    plane.sort(key=lambda item: -hops(item[0]))

    barrier = pltpu.get_barrier_semaphore()
    for o, dc in plane:
        gg, yy = peer(*offsets[o], dc)
        pl.semaphore_signal(barrier, inc=1, device_id=(gg, z * lo + yy), device_id_type=MESH)
    near = level(zh * pair + 1 - zl)
    far_mid = level((1 - zh) * pair + zh)
    far_end = level((1 - zh) * pair + 1 - zh)
    pl.semaphore_signal(barrier, inc=1, device_id=near, device_id_type=MESH)
    pl.semaphore_signal(barrier, inc=1, device_id=far_mid, device_id_type=MESH)

    @pl.when(is_mid)
    def _():
        pl.semaphore_signal(barrier, inc=1, device_id=far_end, device_id_type=MESH)

    load_s = pltpu.make_async_copy(s_hbm, s_ref, in_sem.at[0])

    def x_copy(h, gg):
        start = (gg * hi + half_of(h) * pair) * lo * block * 2
        return pltpu.make_async_copy(
            x_hbm.at[pl.ds(pl.multiple_of(start, 16), plan.rows_h * 2), :], x_ref.at[h, gg], in_sem.at[2 + h]
        )

    def w_copy(c):
        return pltpu.make_async_copy(w_hbm.at[:, pl.ds(c * cols, cols)], wbuf.at[c, 0], w_sem.at[c])

    w_copy(0).start()
    load_s.start()
    for gg in range(plan.grp):
        x_copy(0, gg).start()
    for c in range(1, chunks):
        w_copy(c).start()
    for gg in range(plan.grp):
        x_copy(1, gg).start()
    load_list = pltpu.make_async_copy(list_hbm, list_ref, in_sem.at[1])
    load_list.start()

    contract = (((1,), (1,)), ((), ()))

    def stack():
        load_s.wait()
        upper = s_ref[...]
        both_buf[...] = jnp.concatenate([upper, -upper[half:], upper[:half]], axis=0)

    def partial(h):
        both = both_buf[...]
        arrived(x_ref.at[h], in_sem.at[2 + h])
        for gg in range(plan.grp):
            value = lax.dot_general(x_ref[h, gg], both, contract, preferred_element_type=F32)
            b = gg % 2
            even_buf[b] = value[:, :width]
            odd_buf[b] = value[:, width:]
            value = (
                even_buf[b, pl.ds(0, plan.rows_h, stride=2), :] + odd_buf[b, pl.ds(1, plan.rows_h, stride=2), :]
            )
            pall[h, gg] = value.reshape(pair, lo, block, width).astype(BF16)

    def remote(src, dst, send, recv, target):
        return pltpu.make_async_remote_copy(
            src_ref=src, dst_ref=dst, send_sem=send, recv_sem=recv, device_id=target, device_id_type=MESH
        )

    def arrived(ref, sem):
        pltpu.make_async_copy(ref, ref, sem).wait()

    def send_w(c):
        w_copy(c).wait()
        for o in sorted(range(count), key=lambda o: -hops(o)):
            if o == 0 and cores == 1:
                continue
            dc = cores - 1
            gg, yy = peer(*offsets[o], dc)
            k = slot(o, dc)
            sem = wrecv.at[c, 1 if o == 0 else 0]
            remote(wbuf.at[c, 0], wbuf.at[c, k], send_sem.at[0], sem, (gg, z * lo + yy)).start()

    def relay_w(c):
        arrived(wbuf.at[c, pl.ds(slot(1, cores - 1), count - 1)], wrecv.at[c, 0])
        if cores == 1:
            return
        gg, yy = peer(0, 0, 1)
        for o in range(1, count):
            source = wbuf.at[c, slot(o, 1)]
            remote(source, wbuf.at[c, o], send_sem.at[0], wrecv.at[c, 1], (gg, z * lo + yy)).start()

    def ready_w(c):
        if cores > 1:
            arrived(wbuf.at[c, pl.ds(1, count)], wrecv.at[c, 1])

    def send_p(h):
        for o, dc in plane:
            gg, yy = peer(*offsets[o], dc)
            k = slot(o, dc)
            source = pall.at[h, gg, :, yy]
            remote(source, pbuf.at[h, k], send_sem.at[1], precv.at[h], (gg, z * lo + yy)).start()

    sign = jnp.where(lax.broadcasted_iota(jnp.int32, (block, width), 1) < half, 1.0, -1.0).astype(F32)
    orders = ((1 - zh, zh), (1 - zl, zl))

    def place(h, k, rows):
        for i in range(pair):
            row = (h * pair + i) * 2 * block
            part = rows(i).astype(F32)
            columns = pl.ds(k * width, width)
            lhs_buf[pl.ds(row, block), columns] = (part * sign).astype(BF16)
            turned = jnp.concatenate([part[:, half:], part[:, :half]], axis=1)
            lhs_buf[pl.ds(row + block, block), columns] = turned.astype(BF16)

    def wait_p(h):
        place(h, 0, lambda i: pall[h, g, orders[h][i], y])
        arrived(pbuf.at[h, pl.ds(1, plan.slots - 1)], precv.at[h])
        for o, dc in plane:
            k = slot(o, dc)
            place(h, k, lambda i: pbuf[h, k, orders[h][i]])

    def product(h, c):
        weights = wbuf[c].reshape(plan.slots * width, cols)
        left = lhs_buf[pl.ds(h * pair * 2 * block, pair * 2 * block), :]
        return jnp.dot(left, weights, preferred_element_type=F32).reshape(pair, 2, block, cols)

    def to_near(c, i):
        return remote(share_buf.at[c, i], near_buf.at[c, i], send_sem.at[2], nrecv.at[c, i], near)

    def to_owner(c, i):
        target = level((1 - zh) * pair + orders[0][i])
        return remote(share_buf.at[c, i], got_buf.at[c, 1], send_sem.at[2], mrecv.at[c], target)

    def to_pair(c):
        return remote(pass_buf.at[c], got_buf.at[c, 0], send_sem.at[3], srecv.at[c], near)

    def first_end(c):
        share_buf[c] = product(0, c).astype(BF16)
        for i in range(pair):
            to_near(c, i).start()

    def first_mid(c):
        own_buf[c] = product(0, c)

    def merge(c):
        for i in range(pair):
            arrived(near_buf.at[c, i], nrecv.at[c, i])
            share_buf[c, i] = (own_buf[c, i] + near_buf[c, i].astype(F32)).astype(BF16)
            to_owner(c, i).start()

    def second(c):
        value = product(1, c)
        pass_buf[c] = value[0].astype(BF16)
        to_pair(c).start()
        last_buf[c] = value[1]

    def finish(c):
        arrived(got_buf.at[c, 1], mrecv.at[c])
        total = last_buf[c] + got_buf[c, 1].astype(F32)
        arrived(got_buf.at[c, 0], srecv.at[c])
        total = total + got_buf[c, 0].astype(F32)
        rounded = total.astype(BF16).reshape(2 * block, cols)
        placed = jnp.dot(rounded, pick_buf[pl.ds(c * cols, cols), :], preferred_element_type=F32)
        if c == 0:
            acc_buf[...] = placed
        elif c < chunks - 1:
            acc_buf[...] += placed
        else:
            out_ref[...] = (acc_buf[...] + placed).astype(BF16).reshape(2, block, plan.beams)

    pl.semaphore_wait(barrier, len(plane) + jnp.where(is_mid, 3, 2))
    for c in range(min(PRE, chunks)):
        send_w(c)
    stack()
    partial(0)
    send_p(0)
    for c in range(min(PRE, chunks), min(AHEAD, chunks)):
        send_w(c)
    partial(1)
    load_list.wait()
    for c in range(chunks):
        row = lax.broadcasted_iota(jnp.int32, (cols, plan.beams), 0) + c * cols
        pick_buf[pl.ds(c * cols, cols), :] = jnp.where(row == list_ref[...], 1.0, 0.0).astype(BF16)
    actions = {
        "W": send_w,
        "R": relay_w,
        "Y": ready_w,
        "M": merge,
        "P": wait_p,
        "S": second,
    }

    def follow(steps, first):
        for step in steps:
            if step == "X":
                send_p(1)
            elif step[0] == "F":
                first(int(step[1:]))
            else:
                actions[step[0]](int(step[1:]))

    @pl.when(is_end)
    def _():
        follow(plan.steps(END), first_end)

    @pl.when(is_mid)
    def _():
        follow(plan.steps(MID), first_mid)

    arrived(wbuf.at[:, pl.ds(1, plan.slots - 1)], send_sem.at[0])
    arrived(pbuf.at[:, pl.ds(1, plan.slots - 1)], send_sem.at[1])
    for c in range(chunks):
        if c == chunks - 1:
            arrived(share_buf, send_sem.at[2])
            arrived(pass_buf, send_sem.at[3])
        finish(c)


def shards(plan, snapshots, steering, combining, beam_list):
    snap, _, _, elements = snapshots.shape
    signal = snapshots.reshape(snap * 2, elements)
    steer = jnp.transpose(steering[0], (0, 2, 1)).reshape(plan.width, elements)
    weights = combining.reshape(plan.width, plan.beams)
    pair, block, cols, chunks, halves = plan.pair, plan.block, plan.cols, plan.chunks, plan.halves
    hbm = pl.BlockSpec(memory_space=pl.ANY)
    dma = pltpu.SemaphoreType.DMA
    return pl.pallas_call(
        functools.partial(beam_kernel, plan),
        out_shape=pltpu.VMEM((2, block, plan.beams), BF16),
        in_specs=[hbm, hbm, hbm, hbm],
        out_specs=pl.BlockSpec(memory_space=pltpu.VMEM),
        scratch_shapes=[
            pltpu.VMEM((halves, plan.grp, plan.rows_h * 2, elements), BF16),
            pltpu.VMEM((plan.width, elements), BF16),
            pltpu.VMEM((2 * plan.width, elements), BF16),
            pltpu.VMEM((1, plan.beams), jnp.int32),
            dma((2 + halves,)),
            dma((chunks,)),
            pltpu.VMEM((2, plan.rows_h * 2, plan.width), F32),
            pltpu.VMEM((2, plan.rows_h * 2, plan.width), F32),
            pltpu.VMEM((halves, plan.grp, pair, plan.lo, block, plan.width), BF16),
            pltpu.VMEM((halves, plan.slots, pair, block, plan.width), BF16),
            pltpu.VMEM((halves * pair * 2 * block, plan.slots * plan.width), BF16),
            pltpu.VMEM((chunks, plan.slots, plan.width, cols), BF16),
            pltpu.VMEM((chunks, pair, 2, block, cols), F32),
            pltpu.VMEM((chunks, pair, 2, block, cols), BF16),
            pltpu.VMEM((chunks, 2, block, cols), BF16),
            pltpu.VMEM((chunks, 2, block, cols), F32),
            pltpu.VMEM((chunks, pair, 2, block, cols), BF16),
            pltpu.VMEM((chunks, 2, 2, block, cols), BF16),
            pltpu.VMEM((plan.beams, plan.beams), BF16),
            pltpu.VMEM((2 * block, plan.beams), F32),
            dma((4,)),
            dma((halves,)),
            dma((chunks, 2)),
            dma((chunks,)),
            dma((chunks,)),
            dma((chunks, pair)),
        ],
        compiler_params=pltpu.CompilerParams(
            collective_id=0, has_side_effects=True, vmem_limit_bytes=VMEM_LIMIT
        ),
    )(signal, steer, weights, beam_list.reshape(1, plan.beams))


def solution(mesh):
    placed = (
        P(None, None, ("grp", "sub"), None),
        P(("grp", "sub"), None, None, None),
        P(("grp", "sub"), None, None, None),
        P(),
    )

    def whole(snapshots, steering, combining, beam_list):
        plan = Plan(mesh, snapshots.shape[0], 2 * steering.shape[3], combining.shape[3])
        return jax.shard_map(
            functools.partial(shards, plan),
            mesh=mesh,
            in_specs=placed,
            out_specs=P(None, ("grp", "sub"), None),
            check_vma=False,
        )(snapshots, steering, combining, beam_list)

    return whole
```

time: 42.3 us -> 33.2 us (0.78)
  Pallas kernels: 40.5 us -> 32.4 us
  local copies, waits for them, and re-layouts: 1.67 us -> 0.71 us
    pallas_call x1, Pallas kernels: 40.5 us -> 32.4 us  [shards(): pl.pallas_call(functools.partial(beam_kernel, plan), out_shape=pltpu.VMEM...]
    unnamed x1, local copies, waits for them, and re-layouts: 1.67 us -> 0.71 us
where the time goes in v2:
time: 33.2 us; the launch traced here: 33.1 us
  Pallas kernels  32.4 us (98%)
  local copies, waits for them, and re-layouts  0.71 us (2%)
    pallas_call x1, Pallas kernels, shards(): pl.pallas_call(functools.partial(beam_kernel, plan), out_shape=pltpu.VMEM...  32.4 us
    unnamed x1, local copies, waits for them, and re-layouts  0.71 us

profile of v2, /device:TPU:0, one launch (start us, length us, event | category | flops | bytes accessed | tf_op | source)
XLA Modules:
  0.0 33.1 jit_solution(12668852880892754802)
XLA Ops:
  0.0 32.4 %shard_map.46 = bf16[2,64,1024]{2,1,0:T(8,128)(2,1)S(1)} custom-call(bf16[4096,128]{1,0:T(8,128)(2,1)} %bitcast.8, bf16[128,128]{1,0:T(8,128)(2,1)} %bitcast.10, bf16[128,1024]{1,0:T(8,128)(2,1)} %bitcast.9, s32[1,1024]{1,0:T(1,128)} %bitcast.11), custom_call_target="tpu_custom_call" | custom-call | tf_op jit(solution)/shard_map/pallas_call | solution.py:423
  32.4 0.7 %copy.6 = bf16[2,64,1024]{2,1,0:T(8,128)(2,1)} copy(bf16[2,64,1024]{2,1,0:T(8,128)(2,1)S(1)} %shard_map.46) | data formatting | bytes 524288

commit v3 on v2

--- a/solution.py
+++ b/solution.py
@@ -66,41 +66,41 @@
     "R1",
     "Y1",
     "F1",
+    "M0",
     "R2",
     "Y2",
     "F2",
-    "M0",
     "R3",
+    "M1",
     "Y3",
     "F3",
-    "M1",
     "R4",
+    "M2",
     "Y4",
     "F4",
-    "M2",
     "P1",
     "S0",
+    "S1",
     "M3",
     "R5",
-    "S1",
+    "S2",
+    "S3",
     "M4",
-    "S2",
     "Y5",
     "F5",
     "R6",
-    "S3",
+    "S4",
     "M5",
-    "S4",
     "Y6",
     "F6",
     "R7",
     "S5",
+    "S6",
     "M6",
-    "S6",
     "Y7",
     "F7",
+    "M7",
     "S7",
-    "M7",
 ]
 VMEM_LIMIT = 60 * 1024 * 1024
 
@@ -145,7 +145,7 @@
     both_buf,
     list_ref,
     in_sem,
-    w_sem,
+    list_sem,
     even_buf,
     odd_buf,
     pall,
@@ -164,7 +164,6 @@
     precv,
     wrecv,
     srecv,
-    mrecv,
     nrecv,
 ):
     cores, nx, lo, hi = plan.cores, plan.nx, plan.lo, plan.hi
@@ -224,7 +223,7 @@
         )
 
     def w_copy(c):
-        return pltpu.make_async_copy(w_hbm.at[:, pl.ds(c * cols, cols)], wbuf.at[c, 0], w_sem.at[c])
+        return pltpu.make_async_copy(w_hbm.at[:, pl.ds(c * cols, cols)], wbuf.at[c, 0], in_sem.at[4 if c else 1])
 
     w_copy(0).start()
     load_s.start()
@@ -234,7 +233,7 @@
         w_copy(c).start()
     for gg in range(plan.grp):
         x_copy(1, gg).start()
-    load_list = pltpu.make_async_copy(list_hbm, list_ref, in_sem.at[1])
+    load_list = pltpu.make_async_copy(list_hbm, list_ref, list_sem)
     load_list.start()
 
     contract = (((1,), (1,)), ((), ()))
@@ -266,7 +265,10 @@
         pltpu.make_async_copy(ref, ref, sem).wait()
 
     def send_w(c):
-        w_copy(c).wait()
+        if c == 0:
+            w_copy(0).wait()
+        if c == 1:
+            arrived(wbuf.at[pl.ds(1, chunks - 1), 0], in_sem.at[4])
         for o in sorted(range(count), key=lambda o: -hops(o)):
             if o == 0 and cores == 1:
                 continue
@@ -321,11 +323,11 @@
         return jnp.dot(left, weights, preferred_element_type=F32).reshape(pair, 2, block, cols)
 
     def to_near(c, i):
-        return remote(share_buf.at[c, i], near_buf.at[c, i], send_sem.at[2], nrecv.at[c, i], near)
+        return remote(share_buf.at[c, i], near_buf.at[c, i], send_sem.at[2], nrecv.at[c + i if c == chunks - 1 else c], near)
 
     def to_owner(c, i):
         target = level((1 - zh) * pair + orders[0][i])
-        return remote(share_buf.at[c, i], got_buf.at[c, 1], send_sem.at[2], mrecv.at[c], target)
+        return remote(share_buf.at[c, i], got_buf.at[c, 1], send_sem.at[2], srecv.at[c], target)
 
     def to_pair(c):
         return remote(pass_buf.at[c], got_buf.at[c, 0], send_sem.at[3], srecv.at[c], near)
@@ -339,8 +341,11 @@
         own_buf[c] = product(0, c)
 
     def merge(c):
+        if c < chunks - 1:
+            arrived(near_buf.at[c], nrecv.at[c])
         for i in range(pair):
-            arrived(near_buf.at[c, i], nrecv.at[c, i])
+            if c == chunks - 1:
+                arrived(near_buf.at[c, i], nrecv.at[c + i])
             share_buf[c, i] = (own_buf[c, i] + near_buf[c, i].astype(F32)).astype(BF16)
             to_owner(c, i).start()
 
@@ -351,10 +356,8 @@
         last_buf[c] = value[1]
 
     def finish(c):
-        arrived(got_buf.at[c, 1], mrecv.at[c])
-        total = last_buf[c] + got_buf[c, 1].astype(F32)
-        arrived(got_buf.at[c, 0], srecv.at[c])
-        total = total + got_buf[c, 0].astype(F32)
+        arrived(got_buf.at[c], srecv.at[c])
+        total = last_buf[c] + got_buf[c, 1].astype(F32) + got_buf[c, 0].astype(F32)
         rounded = total.astype(BF16).reshape(2 * block, cols)
         placed = jnp.dot(rounded, pick_buf[pl.ds(c * cols, cols), :], preferred_element_type=F32)
         if c == 0:
@@ -430,8 +433,8 @@
             pltpu.VMEM((plan.width, elements), BF16),
             pltpu.VMEM((2 * plan.width, elements), BF16),
             pltpu.VMEM((1, plan.beams), jnp.int32),
-            dma((2 + halves,)),
-            dma((chunks,)),
+            dma((5,)),
+            dma(()),
             pltpu.VMEM((2, plan.rows_h * 2, plan.width), F32),
             pltpu.VMEM((2, plan.rows_h * 2, plan.width), F32),
             pltpu.VMEM((halves, plan.grp, pair, plan.lo, block, plan.width), BF16),
@@ -450,8 +453,7 @@
             dma((halves,)),
             dma((chunks, 2)),
             dma((chunks,)),
-            dma((chunks,)),
-            dma((chunks, pair)),
+            dma((chunks + 1,)),
         ],
         compiler_params=pltpu.CompilerParams(
             collective_id=0, has_side_effects=True, vmem_limit_bytes=VMEM_LIMIT

time: 33.2 us -> 33.1 us (level)
  no operation moved by 1% of the time
where the time goes in v3:
time: 33.1 us; the launch traced here: 32.9 us
  Pallas kernels  32.2 us (97%)
  local copies, waits for them, and re-layouts  0.71 us (2%)
    pallas_call x1, Pallas kernels, shards(): pl.pallas_call(functools.partial(beam_kernel, plan), out_shape=pltpu.VMEM...  32.2 us
    unnamed x1, local copies, waits for them, and re-layouts  0.71 us

profile of v3, /device:TPU:0, one launch (start us, length us, event | category | flops | bytes accessed | tf_op | source)
XLA Modules:
  0.0 32.9 jit_solution(2682853025394338806)
XLA Ops:
  0.0 32.2 %shard_map.46 = bf16[2,64,1024]{2,1,0:T(8,128)(2,1)S(1)} custom-call(bf16[4096,128]{1,0:T(8,128)(2,1)} %bitcast.8, bf16[128,128]{1,0:T(8,128)(2,1)} %bitcast.10, bf16[128,1024]{1,0:T(8,128)(2,1)} %bitcast.9, s32[1,1024]{1,0:T(1,128)} %bitcast.11), custom_call_target="tpu_custom_call" | custom-call | tf_op jit(solution)/shard_map/pallas_call | solution.py:426
  32.2 0.7 %copy.6 = bf16[2,64,1024]{2,1,0:T(8,128)(2,1)} copy(bf16[2,64,1024]{2,1,0:T(8,128)(2,1)S(1)} %shard_map.46) | data formatting | bytes 524288

commit v4 on v3

--- a/solution.py
+++ b/solution.py
@@ -368,12 +368,19 @@
             out_ref[...] = (acc_buf[...] + placed).astype(BF16).reshape(2, block, plan.beams)
 
     pl.semaphore_wait(barrier, len(plane) + jnp.where(is_mid, 3, 2))
-    for c in range(min(PRE, chunks)):
-        send_w(c)
+    @pl.when(core == 0)
+    def _():
+        send_w(0)
+
     stack()
     partial(0)
     send_p(0)
-    for c in range(min(PRE, chunks), min(AHEAD, chunks)):
+
+    @pl.when(core != 0)
+    def _():
+        send_w(0)
+
+    for c in range(1, min(AHEAD, chunks)):
         send_w(c)
     partial(1)
     load_list.wait()

time: 33.1 us -> 33.2 us (level)
  no operation moved by 1% of the time
where the time goes in v4:
time: 33.2 us; the launch traced here: 33.1 us
  Pallas kernels  32.4 us (98%)
  local copies, waits for them, and re-layouts  0.71 us (2%)
    pallas_call x1, Pallas kernels, shards(): pl.pallas_call(functools.partial(beam_kernel, plan), out_shape=pltpu.VMEM...  32.4 us
    unnamed x1, local copies, waits for them, and re-layouts  0.71 us

profile of v4, /device:TPU:0, one launch (start us, length us, event | category | flops | bytes accessed | tf_op | source)
XLA Modules:
  0.0 33.1 jit_solution(7426303624888333084)
XLA Ops:
  0.0 32.4 %shard_map.46 = bf16[2,64,1024]{2,1,0:T(8,128)(2,1)S(1)} custom-call(bf16[4096,128]{1,0:T(8,128)(2,1)} %bitcast.8, bf16[128,128]{1,0:T(8,128)(2,1)} %bitcast.10, bf16[128,1024]{1,0:T(8,128)(2,1)} %bitcast.9, s32[1,1024]{1,0:T(1,128)} %bitcast.11), custom_call_target="tpu_custom_call" | custom-call | tf_op jit(solution)/shard_map/pallas_call | solution.py:433
  32.4 0.7 %copy.6 = bf16[2,64,1024]{2,1,0:T(8,128)(2,1)} copy(bf16[2,64,1024]{2,1,0:T(8,128)(2,1)S(1)} %shard_map.46) | data formatting | bytes 524288
